TPU v7x, 32 devices: a whole 2x2x4 slice. The times are simulated.
32 devices in a mesh: dp: 16 (over z, y, x), tensor: 2 (over core).
Axes of the slice: x: 2, y: 2, z: 4, core: 2. Of those that a mesh axis runs over, the one named last changes fastest.
Arguments:
- tokens: bfloat16 [16384, 768], P(('dp', 'tensor')), may hold values from -6 to 6
- cotangent: bfloat16 [16384, 768], P(('dp', 'tensor')), may hold values from -6 to 6
- prefix: int32 [16], P('dp'), may hold values from 102 to 512, as said below
- routes: int32 [16384, 1], P('dp'), may hold values from 0 to 1; in each aligned block of 1024 rows (0 to 1023, 1024 to 2047, ...) at most 640 rows name the same one
- norm1_gain: float32 [768], P(('dp', 'tensor')), may hold values from 0.5 to 1.5
- norm1_bias: float32 [768], P(('dp', 'tensor')), may hold values from -0.625 to 0.625
- w_query: bfloat16 [768, 768], P('dp', 'tensor'), may hold values from -0.4375 to 0.4375
- w_key: bfloat16 [768, 768], P('dp', 'tensor'), may hold values from -0.21875 to 0.21875
- w_value: bfloat16 [768, 768], P('dp', 'tensor'), may hold values from -0.21875 to 0.21875
- w_out: bfloat16 [768, 768], P('tensor', 'dp'), may hold values from -1.75 to 1.75
- norm2_gain: float32 [768], P(('dp', 'tensor')), may hold values from 0.5 to 1.5
- norm2_bias: float32 [768], P(('dp', 'tensor')), may hold values from -0.625 to 0.625
- centroids: float32 [2, 768], P(None, ('dp', 'tensor')), may hold values from -0.1875 to 0.1875
- expert_in: bfloat16 [2, 768, 3072], P(None, 'dp', 'tensor'), may hold values from -0.21875 to 0.21875
- expert_out: bfloat16 [2, 3072, 768], P(None, 'tensor', 'dp'), may hold values from -0.4375 to 0.4375
Outputs:
- block_out: bfloat16 [16384, 768], P(('dp', 'tensor'))
- grad_tokens: bfloat16 [16384, 768], P(('dp', 'tensor'))
- grad_norm1_gain: float32 [768], P(('dp', 'tensor'))
- grad_norm1_bias: float32 [768], P(('dp', 'tensor'))
- grad_w_query: float32 [768, 768], P('dp', 'tensor')
- grad_w_key: float32 [768, 768], P('dp', 'tensor')
- grad_w_value: float32 [768, 768], P('dp', 'tensor')
- grad_w_out: float32 [768, 768], P('tensor', 'dp')
- grad_norm2_gain: float32 [768], P(('dp', 'tensor'))
- grad_norm2_bias: float32 [768], P(('dp', 'tensor'))
- grad_centroids: float32 [2, 768], P(None, ('dp', 'tensor'))
- grad_expert_in: float32 [2, 768, 3072], P(None, 'dp', 'tensor')
- grad_expert_out: float32 [2, 3072, 768], P(None, 'tensor', 'dp')
Inputs may be any that keep to these rules, and one draw needn't show every extreme that they name: Each sequence's first prefix tokens see one another; some sequence's prefix is exactly half of 1024. `routes`: in each aligned block of 1024 rows (the tokens of one index of dp) no expert is named by more than 640 rows; some block names an expert exactly 640 times.
All inputs are finite; a program needn't handle non-finite values.
Results may differ from a plain program's by a relative error of at most 0.02.
Values may be sent and summed in bfloat16 or wider, within the bound.
A program may use at most 192 MiB of HBM per device.

v0:
```python
import functools

import jax
import jax.numpy as jnp
from jax import lax
from jax.experimental import pallas as pl
from jax.experimental.pallas import tpu as pltpu
from jax.sharding import PartitionSpec as P


HEADS = 12
CAP = 640
EPS = 1e-05
NEGATIVE = -1e30
BF = jnp.bfloat16
F32 = jnp.float32
MESH = pl.DeviceIdType.MESH


def factors_of(count):
    rest, sizes = count // 2, []
    while rest % 4 == 0:
        sizes.append(4)
        rest //= 4
    while rest % 2 == 0 and rest > 1:
        sizes.append(2)
        rest //= 2
    return sizes + ([2] if count > 1 else [])


class Ring:
    def __init__(self, count):
        self.count = count
        self.sizes = factors_of(count)
        self.strides = []
        stride = count
        for size in self.sizes:
            stride //= size
            self.strides.append(stride)
        self.square = len(self.sizes) >= 2 and self.sizes[-1] == 2 and self.sizes[-2] == 2

    def order(self, size):
        return [0, 1, 3, 2] if size == 4 else list(range(size))

    def shift(self, stage, step):
        size, stride = self.sizes[stage], self.strides[stage]
        order = self.order(size)
        pairs = []
        for source in range(self.count):
            digit = source // stride % size
            target = order[(order.index(digit) + step) % size]
            pairs.append((source, source + (target - digit) * stride))
        return pairs

    def move(self, value, stage, step):
        return lax.ppermute(value, "dp", self.shift(stage, step))

    def lead(self, block):
        for stage in range(len(self.sizes) - (2 if self.square else 0)):
            parts = [block] + [self.move(block, stage, s) for s in range(1, self.sizes[stage])]
            block = jnp.concatenate(parts, axis=0)
        return lax.optimization_barrier(block)

    def cross(self, block):
        if not self.square:
            return ()
        y, x = len(self.sizes) - 2, len(self.sizes) - 1
        return self.move(block, x, 1), self.move(block, y, 1)

    def close(self, block, crossed):
        if not self.square:
            return block
        y, x = len(self.sizes) - 2, len(self.sizes) - 1
        half = block.shape[0] // 2
        from_x, from_y = crossed
        low, high = self.move(from_y[:half], x, 1), self.move(from_x[half:], y, 1)
        return jnp.concatenate([block, from_y, from_x, low, high], axis=0)

    def along(self, blocks):
        steps = [blocks] + [self.move(blocks, 0, step) for step in range(1, 4)]
        rows, width = blocks.shape
        joined = jnp.stack([step.reshape(4, rows // 4, width) for step in steps], axis=1)
        return joined.reshape(4 * rows, width)

    def gather(self, block):
        block = self.lead(block)
        return self.close(block, self.cross(block))

    def far(self, total, kind):
        if not self.square:
            return ()
        y, x = len(self.sizes) - 2, len(self.sizes) - 1
        quarter = total.shape[0] // 4
        half = quarter // 2
        far = total[3 * quarter :]
        return self.move(far[:half].astype(kind), x, 1), self.move(far[half:].astype(kind), y, 1)

    def near(self, total, via, kind):
        if not self.square:
            return ()
        y, x = len(self.sizes) - 2, len(self.sizes) - 1
        quarter = total.shape[0] // 4
        half = quarter // 2
        via_x, via_y = via
        to_y, to_x = total[quarter : 2 * quarter], total[2 * quarter : 3 * quarter]
        to_y = jnp.concatenate([(to_y[:half].astype(F32) + via_x).astype(kind), to_y[half:].astype(kind)], axis=0)
        to_x = jnp.concatenate([to_x[:half].astype(kind), (to_x[half:].astype(F32) + via_y).astype(kind)], axis=0)
        return self.move(to_x, x, 1), self.move(to_y, y, 1)

    def last(self, total, crossed, kind):
        stages = len(self.sizes)
        if self.square:
            own = total[: total.shape[0] // 4].astype(F32)
            total = own + crossed[0].astype(F32) + crossed[1].astype(F32)
            stages -= 2
        for stage in reversed(range(stages)):
            size = self.sizes[stage]
            piece = total.shape[0] // size
            parts = [total[i * piece : (i + 1) * piece] for i in range(size)]
            total = parts[0].astype(F32)
            for step in range(1, size):
                total = total + self.move(parts[step].astype(kind), stage, size - step).astype(F32)
        return total

    def scatter(self, total, kind):
        return self.last(total, self.near(total, self.far(total, kind), kind), kind)

    def width_order(self, width):
        me = lax.axis_index("dp")
        rows = width // self.count
        column = jnp.arange(width, dtype=jnp.int32)
        inner, block = column % rows, column // rows
        found = jnp.zeros_like(column)
        for size, stride in zip(self.sizes, self.strides):
            step, block = block % size, block // size
            digit = me // stride % size
            if size == 4:
                place = jnp.bitwise_xor(digit, digit // 2)
                back = (place - step + size) % size
                source = jnp.bitwise_xor(back, back // 2)
            else:
                source = (digit - step + size) % size
            found = found + source * stride
        return found * rows + inner


def ring_place(digit):
    return digit + (digit // 2) * (1 - 2 * (digit % 2))


def partners_of(me):
    digit = me // 4
    place = ring_place(digit)
    along = [me + (ring_place((place + step) % 4) - digit) * 4 for step in range(1, 4)]
    return along, me + 1 - 2 * (me % 2), me + 2 - 4 * ((me // 2) % 2)


def greet(along, x_way, y_way, other):
    barrier = pltpu.get_barrier_semaphore()
    for device in along + [x_way, y_way]:
        pl.semaphore_signal(barrier, inc=1, device_id={"dp": device}, device_id_type=MESH)
    pl.semaphore_signal(barrier, inc=1, device_id={"tensor": other}, device_id_type=MESH)
    pl.semaphore_wait(barrier, 6)


CHUNK = 16


def gather_kernel(vec_ref, qkv_ref, vec_out, qkv_out, vec_other, send, recv, local):
    along, x_way, y_way = partners_of(lax.axis_index("dp"))
    other = 1 - lax.axis_index("tensor")
    greet(along, x_way, y_way, other)
    kinds = 1 + qkv_ref.shape[0] // CHUNK
    copies = {}

    def own(kind):
        return qkv_ref.at[pl.ds((kind - 1) * CHUNK, CHUNK)] if kind else vec_ref

    def slot_of(kind, slot):
        return qkv_out.at[slot, pl.ds((kind - 1) * CHUNK, CHUNK)] if kind else vec_out.at[slot]

    def start(kind, source, slot, device):
        copy = pltpu.make_async_remote_copy(
            src_ref=source,
            dst_ref=slot_of(kind, slot),
            send_sem=send.at[kind, slot],
            recv_sem=recv.at[kind, slot],
            device_id={"dp": device},
            device_id_type=MESH,
        )
        copy.start()
        copies[kind, slot] = copy

    def pass_far(kind):
        for step in range(4):
            slot = 4 + step if step < 2 else 8 + step
            copies[kind, slot].wait_recv()
            start(kind, slot_of(kind, slot), 12 + step, x_way if step < 2 else y_way)

    kept = []
    for kind in range(kinds):
        for step in range(1, 4):
            start(kind, own(kind), step, along[step - 1])
        start(kind, own(kind), 4, y_way)
        start(kind, own(kind), 8, x_way)
        copy = pltpu.make_async_copy(own(kind), slot_of(kind, 0), local.at[kind])
        copy.start()
        kept.append(copy)
    for kind in range(kinds):
        for step in range(1, 4):
            copies[kind, step].wait_recv()
            start(kind, slot_of(kind, step), 4 + step, y_way)
            start(kind, slot_of(kind, step), 8 + step, x_way)
        if kind:
            pass_far(kind - 1)
    pass_far(kinds - 1)
    rest = (6, 7, 8, 9, 12, 13, 14, 15)
    for slot in rest:
        copies[0, slot].wait_recv()
    kept[0].wait()
    shared = pltpu.make_async_remote_copy(
        src_ref=vec_out,
        dst_ref=vec_other,
        send_sem=send.at[0, 0],
        recv_sem=recv.at[0, 0],
        device_id={"tensor": other},
        device_id_type=MESH,
    )
    shared.start()
    for kind in range(1, kinds):
        for slot in rest:
            copies[kind, slot].wait_recv()
        kept[kind].wait()
    for copy in copies.values():
        copy.wait_send()
    shared.wait()


def gather_first(vectors, qkv):
    anywhere = pl.BlockSpec(memory_space=pl.ANY)
    inside = pl.BlockSpec(memory_space=pltpu.VMEM)
    kinds = 1 + qkv.shape[0] // CHUNK
    return pl.pallas_call(
        gather_kernel,
        out_shape=(
            jax.ShapeDtypeStruct((16, *vectors.shape), vectors.dtype),
            jax.ShapeDtypeStruct((16, *qkv.shape), qkv.dtype),
            jax.ShapeDtypeStruct((16, *vectors.shape), vectors.dtype),
        ),
        in_specs=[inside, inside],
        out_specs=(anywhere, anywhere, anywhere),
        scratch_shapes=[
            pltpu.SemaphoreType.DMA((kinds, 16)),
            pltpu.SemaphoreType.DMA((kinds, 16)),
            pltpu.SemaphoreType.DMA((kinds,)),
        ],
        compiler_params=pltpu.CompilerParams(collective_id=0, has_side_effects=True),
        name="gather_first",
    )(vectors, qkv)


def scatter_kernel(
    small_ref, grad_ref, small_out, grad_out,
    small_via, small_fold, small_cross, small_sums, small_last,
    grad_via, grad_fold, grad_cross, grad_sums, grad_last,
    send, recv,
):
    along, x_way, y_way = partners_of(lax.axis_index("dp"))
    greet(along, x_way, y_way, 1 - lax.axis_index("tensor"))
    kinds = 1 + grad_out.shape[0] // CHUNK
    copies = {}

    def at(pair, kind, slot):
        return pair[1].at[slot, pl.ds((kind - 1) * CHUNK, CHUNK)] if kind else pair[0].at[slot]

    blocks = (small_ref, grad_ref)
    via, fold = (small_via, grad_via), (small_fold, grad_fold)
    cross, sums, last = (small_cross, grad_cross), (small_sums, grad_sums), (small_last, grad_last)

    def wide(pair, kind, slot):
        return at(pair, kind, slot)[...].astype(F32)

    def start(kind, source, target, number, device):
        copy = pltpu.make_async_remote_copy(
            src_ref=source,
            dst_ref=target,
            send_sem=send.at[kind, number],
            recv_sem=recv.at[kind, number],
            device_id={"dp": device},
            device_id_type=MESH,
        )
        copy.start()
        copies[kind, number] = copy

    def result(kind):
        return grad_out.at[pl.ds((kind - 1) * CHUNK, CHUNK)] if kind else small_out

    def close(kind):
        for step in (3, 1, 2, 0):
            copies[kind, 4 + step].wait_recv()
            copies[kind, 8 + step].wait_recv()
            total = wide(blocks, kind, step) + wide(cross, kind, step) + wide(cross, kind, 4 + step)
            if step:
                source = at(sums, kind, step)
                source[...] = total.astype(source.dtype)
                start(kind, source, at(last, kind, step), 12 + step, along[3 - step])
            else:
                result(kind)[...] = total

    for kind in range(kinds):
        for step in range(4):
            way = x_way if step < 2 else y_way
            start(kind, at(blocks, kind, 12 + step), at(via, kind, step), step, way)
        for step in range(2):
            start(kind, at(blocks, kind, 6 + step), at(cross, kind, 2 + step), 6 + step, y_way)
            start(kind, at(blocks, kind, 8 + step), at(cross, kind, 4 + step), 8 + step, x_way)
    for kind in range(kinds):
        for step in (1, 3, 0, 2):
            slot = 4 + step if step < 2 else 8 + step
            copies[kind, step].wait_recv()
            source = at(fold, kind, step)
            source[...] = (wide(blocks, kind, slot) + wide(via, kind, step)).astype(source.dtype)
            start(kind, source, at(cross, kind, slot - 4), slot, y_way if step < 2 else x_way)
        if kind:
            close(kind - 1)
    close(kinds - 1)
    for kind in range(kinds):
        for step in range(1, 4):
            copies[kind, 12 + step].wait_recv()
            result(kind)[...] += wide(last, kind, step)
    for copy in copies.values():
        copy.wait_send()


def scatter_last(small, grads):
    inside = pl.BlockSpec(memory_space=pltpu.VMEM)
    scratch = []
    for value in (small, grads):
        for slots in (4, 4, 8, 4, 4):
            scratch.append(pltpu.VMEM((slots, *value.shape[1:]), value.dtype))
    return pl.pallas_call(
        scatter_kernel,
        out_shape=(
            jax.ShapeDtypeStruct(small.shape[1:], F32),
            jax.ShapeDtypeStruct(grads.shape[1:], F32),
        ),
        in_specs=[inside, inside],
        out_specs=(inside, inside),
        scratch_shapes=scratch
        + [pltpu.SemaphoreType.DMA((1 + grads.shape[1] // CHUNK, 16))] * 2,
        compiler_params=pltpu.CompilerParams(collective_id=1, has_side_effects=True),
        name="scatter_last",
    )(small, grads)


def swap(value):
    return lax.ppermute(value, "tensor", [(0, 1), (1, 0)])


def after(value, earlier):
    return lax.optimization_barrier((value, earlier))[0]


def dot(a, b):
    return lax.dot_general(a, b, (((1,), (0,)), ((), ())), preferred_element_type=F32)


def dot_nt(a, b):
    return lax.dot_general(a, b, (((1,), (1,)), ((), ())), preferred_element_type=F32)


def dot_tn(a, b):
    return lax.dot_general(a, b, (((0,), (0,)), ((), ())), preferred_element_type=F32)


def norm_parts(features):
    average = jnp.mean(features, axis=-1, keepdims=True)
    centered = features - average
    spread = jnp.mean(centered * centered, axis=-1, keepdims=True)
    scale = lax.rsqrt(spread + EPS)
    return centered * scale, scale


def norm_back(grad, normed, scale, gain):
    h = grad * gain
    return scale * (
        h - jnp.mean(h, axis=-1, keepdims=True) - normed * jnp.mean(h * normed, axis=-1, keepdims=True)
    )


STRIP = 256


def strip_scores(keys, queries, first, prefix):
    scores = dot_nt(keys, queries) * (queries.shape[1] ** (-0.5))
    key = lax.broadcasted_iota(jnp.int32, scores.shape, 0)
    query = first + lax.broadcasted_iota(jnp.int32, scores.shape, 1)
    return jnp.where((key <= query) | (key < prefix), scores, NEGATIVE)


def strips(length):
    return [(first, max(length // 2, first + STRIP)) for first in range(0, length, STRIP)]


def attend_kernel(head_dim, prefix_ref, q_ref, k_ref, v_ref, out_ref, lse_ref):
    prefix = prefix_ref[0]
    for head in range(q_ref.shape[1] // head_dim):
        columns = slice(head * head_dim, (head + 1) * head_dim)
        for first, reach in strips(q_ref.shape[0]):
            own = slice(first, first + STRIP)
            scores = strip_scores(k_ref[:reach, columns], q_ref[own, columns], first, prefix)
            top = jnp.max(scores, axis=0, keepdims=True)
            powered = jnp.exp(scores - top)
            total = jnp.sum(powered, axis=0, keepdims=True)
            probabilities = (powered * (1.0 / total)).astype(BF)
            attended = dot_tn(v_ref[:reach, columns], probabilities)
            out_ref[own, columns] = attended.T.astype(BF)
            lse_ref[0, head : head + 1, own] = top + jnp.log(total)


def attend_back_kernel(
    head_dim, prefix_ref, q_ref, k_ref, v_ref, back_ref, lse_ref, out_ref, key_sum, value_sum
):
    prefix = prefix_ref[0]
    score_scale = head_dim ** (-0.5)
    for head in range(q_ref.shape[1] // head_dim):
        columns = slice(head * head_dim, (head + 1) * head_dim)
        for first, reach in reversed(strips(q_ref.shape[0])):
            own = slice(first, first + STRIP)
            keys, queries = k_ref[:reach, columns], q_ref[own, columns]
            back_rows = back_ref[own, columns]
            scores = strip_scores(keys, queries, first, prefix)
            probabilities = jnp.exp(scores - lse_ref[0, head : head + 1, own])
            back_probs = dot_nt(v_ref[:reach, columns], back_rows)
            row_dot = jnp.sum(probabilities * back_probs, axis=0, keepdims=True)
            back_scores = (probabilities * (back_probs - row_dot)).astype(BF)
            out_ref[0, own, columns] = (dot_tn(keys, back_scores) * score_scale).T.astype(BF)
            back_key = dot(back_scores, queries)
            back_value = dot(probabilities.astype(BF), back_rows)
            if reach == q_ref.shape[0]:
                key_sum[...] = back_key
                value_sum[...] = back_value
            else:
                key_sum[:reach, :] += back_key
                value_sum[:reach, :] += back_value
        out_ref[1, :, columns] = (key_sum[...] * score_scale).astype(BF)
        out_ref[2, :, columns] = value_sum[...].astype(BF)


def attend_specs(length, groups):
    joint = [
        pl.BlockSpec((length, 128), lambda i, kind=kind: (0, kind * groups + i)) for kind in range(3)
    ]
    rows = pl.BlockSpec((length, 128), lambda i: (0, i))
    sums = pl.BlockSpec((1, 8, length), lambda i: (i, 0, 0))
    return [pl.BlockSpec(memory_space=pltpu.SMEM)] + joint, rows, sums


def attend(qkv, prefix, head_dim):
    length, part = qkv.shape[0], qkv.shape[1] // 3
    groups = part // 128
    inputs, rows, sums = attend_specs(length, groups)
    work = length * length * part
    return pl.pallas_call(
        functools.partial(attend_kernel, head_dim),
        grid=(groups,),
        out_shape=(
            jax.ShapeDtypeStruct((length, part), BF),
            jax.ShapeDtypeStruct((groups, 8, length), F32),
        ),
        in_specs=inputs,
        out_specs=(rows, sums),
        cost_estimate=pl.CostEstimate(
            flops=4 * work, bytes_accessed=8 * length * part, transcendentals=work // head_dim
        ),
        name="attend",
    )(prefix, qkv, qkv, qkv)


def attend_back(qkv, prefix, back_attended, lse, head_dim):
    length, part = back_attended.shape
    groups = part // 128
    inputs, rows, sums = attend_specs(length, groups)
    work = length * length * part
    return pl.pallas_call(
        functools.partial(attend_back_kernel, head_dim),
        grid=(groups,),
        out_shape=jax.ShapeDtypeStruct((3, length, part), BF),
        in_specs=inputs + [rows, sums],
        out_specs=pl.BlockSpec((3, length, 128), lambda i: (0, 0, i)),
        scratch_shapes=[pltpu.VMEM((length, head_dim), F32), pltpu.VMEM((length, head_dim), F32)],
        cost_estimate=pl.CostEstimate(
            flops=10 * work, bytes_accessed=14 * length * part, transcendentals=work // head_dim
        ),
        name="attend_back",
    )(prefix, qkv, qkv, qkv, back_attended, lse)


def body(
    ring,
    tokens,
    cotangent,
    prefix,
    routes,
    norm1_gain,
    norm1_bias,
    w_query,
    w_key,
    w_value,
    w_out,
    norm2_gain,
    norm2_bias,
    centroids,
    expert_in,
    expert_out,
):
    side = lax.axis_index("tensor")
    own_rows, width = tokens.shape
    all_rows = 2 * own_rows
    head_dim = width // HEADS
    part = w_query.shape[1]
    rows = w_query.shape[0]
    experts, _, hidden = expert_in.shape
    count = ring.count

    def both(own):
        other = swap(own)
        return jnp.where(
            side == 0, jnp.concatenate([own, other], 0), jnp.concatenate([other, own], 0)
        )

    vectors = jnp.concatenate(
        [
            norm1_gain[None],
            norm1_bias[None],
            norm2_gain[None],
            norm2_bias[None],
            centroids,
        ],
        axis=0,
    )
    small_count = vectors.shape[0]
    qkv_block = jnp.concatenate([w_query, w_key, w_value, w_out.T], axis=1)
    in_block = expert_in.transpose(1, 0, 2).reshape(rows, experts * hidden)
    out_blocks = expert_out.transpose(2, 0, 1)
    out_block, turned_block = out_blocks[:, 0], out_blocks[:, 1]
    if count == 16:
        padded = jnp.pad(vectors, ((0, 8 - small_count), (0, 128 - rows // 2)))
        table, qkv_w, other_table = gather_first(padded, qkv_block)
        table, other_table = (t[:, :small_count, : rows // 2] for t in (table, other_table))
        table = jnp.where(
            side == 0,
            jnp.concatenate([table, other_table], 2),
            jnp.concatenate([other_table, table], 2),
        )
        qkv_w = qkv_w.reshape(width, 4 * part)
    else:
        other_vectors = swap(vectors)
        vectors = jnp.where(
            side == 0,
            jnp.concatenate([vectors, other_vectors], 1),
            jnp.concatenate([other_vectors, vectors], 1),
        )
        table = ring.gather(vectors.reshape(1, small_count * rows)).reshape(count, small_count, rows)
        qkv_w = ring.gather(qkv_block)
    table = table.transpose(1, 0, 2).reshape(small_count, width)
    gain_one, bias_one, gain_two, bias_two = (table[i : i + 1] for i in range(4))
    centres = table[4:]

    qkv_w, in_block, turned_block = lax.optimization_barrier((qkv_w, in_block, turned_block))
    qkv_w, out_w = qkv_w[:, : 3 * part], qkv_w[:, 3 * part :]
    in_lead = ring.lead(in_block)
    if count == 16:
        turned_crossed = ring.cross(turned_block)
        turned_square = ring.close(turned_block, turned_crossed)
        in_lead, turned_square = lax.optimization_barrier((in_lead, turned_square))
        turned_w = ring.along(turned_square)
    else:
        turned_w = ring.gather(turned_block)
    in_crossed = ring.cross(in_lead)
    out_lead = ring.lead(after(out_block, in_lead))
    in_w = ring.close(in_lead, in_crossed)
    out_crossed = ring.cross(after(out_lead, in_w))
    back_ws = (ring.close(out_lead, out_crossed), turned_w)

    found = ring.width_order(width)
    to_order = (jnp.arange(width, dtype=jnp.int32)[:, None] == found[None, :]).astype(BF)
    tokens_all = dot(both(tokens), to_order)
    back_all = lax.optimization_barrier(dot(both(cotangent), to_order).astype(BF)).astype(F32)

    normed_one, scale_one = norm_parts(tokens_all)
    first_rows = (normed_one * gain_one + bias_one).astype(BF)
    qkv = dot(first_rows, qkv_w).astype(BF)
    attended, lse = attend(qkv, prefix, head_dim)
    attended = after(attended, in_lead)

    attn_terms = dot_nt(attended, out_w).astype(BF)
    residual = tokens_all + (attn_terms.astype(F32) + swap(attn_terms).astype(F32))
    normed_two, scale_two = norm_parts(residual)
    second_rows = (normed_two * gain_two + bias_two).astype(BF)
    second_wide = second_rows.astype(F32)

    is_last = routes == 1
    ones_before = jnp.tril(jnp.ones((all_rows, all_rows), BF))
    last_before = dot(ones_before, is_last.astype(BF)).astype(jnp.int32)
    position = jnp.arange(all_rows, dtype=jnp.int32)[:, None]
    first_count = all_rows - last_before[all_rows - 1, 0]
    place = jnp.where(is_last, first_count + last_before - 1, position - last_before)
    sort_to = (place == jnp.arange(all_rows, dtype=jnp.int32)[None, :]).astype(BF)
    tail = all_rows - CAP
    in_first = position < first_count

    centre_rows = jnp.where(is_last, centres[1:2], centres[0:1])
    gate = jax.nn.sigmoid(jnp.sum(second_wide * centre_rows, axis=-1, keepdims=True))
    back_branch = (gate * back_all).astype(BF)
    gate, back_branch, sent_rows = lax.optimization_barrier((gate, back_branch, second_rows))
    picked = dot_tn(sort_to, sent_rows).astype(BF)
    back_slots = dot_tn(sort_to, back_branch).astype(BF)
    windows = (slice(0, CAP), slice(tail, all_rows))
    masks = (in_first[:CAP], ~in_first[tail:])
    slot_out, back_picked, grads_in, grads_out = [], [], [], []
    hidden_of = []
    for e in range(2):
        columns = slice(e * hidden, (e + 1) * hidden)
        rows_in = picked[windows[e]]
        back_rows = jnp.where(masks[e], back_slots[windows[e]], jnp.zeros((), BF))
        up = dot(rows_in, in_w[:, columns])
        activated = lax.optimization_barrier(jax.nn.gelu(up).astype(BF))
        grads_out.append(dot_tn(back_rows, activated).astype(BF))
        hidden_of.append((columns, rows_in, back_rows, up, activated))
    grads_out = jnp.concatenate(grads_out, axis=1)
    out_via = ring.far(grads_out, BF)
    for e, (columns, rows_in, back_rows, up, activated) in enumerate(hidden_of):
        if e == 1:
            back_rows = after(back_rows, out_via)
        slot_out.append(dot_nt(activated, back_ws[e]).astype(BF))
        back_activated = dot(back_rows, back_ws[e])
        back_up = jax.vjp(jax.nn.gelu, up)[1](back_activated)[0].astype(BF)
        grads_in.append(dot_tn(rows_in, back_up).astype(BF))
        back_picked.append(dot_nt(back_up, in_w[:, columns]).astype(BF))
    grads_in = jnp.concatenate(grads_in, axis=1)
    out_near = ring.near(grads_out, out_via, BF)
    in_via = ring.far(after(grads_in, out_via), BF)

    def unsort(pieces):
        joined = jnp.concatenate(
            [
                pieces[0][:tail],
                jnp.where(in_first[tail:CAP], pieces[0][tail:], pieces[1][: CAP - tail]),
                pieces[1][CAP - tail :],
            ],
            axis=0,
        )
        return dot(sort_to, joined).astype(BF)

    row_terms = unsort(slot_out)
    expert_rows = row_terms.astype(F32) + swap(row_terms).astype(F32)
    block_all = (residual + gate * expert_rows).astype(BF)
    first_own = side * own_rows
    block_out = dot_nt(lax.dynamic_slice_in_dim(block_all, first_own, own_rows), to_order).astype(BF)
    back_score = jnp.sum(back_all * expert_rows, axis=-1, keepdims=True) * gate * (1.0 - gate)

    second_terms = unsort(back_picked)
    back_second = second_terms.astype(F32) + swap(second_terms).astype(F32) + back_score * centre_rows
    weighted = back_score * second_wide
    grad_centre = jnp.stack(
        [
            jnp.sum(jnp.where(is_last, 0.0, weighted), axis=0),
            jnp.sum(jnp.where(is_last, weighted, 0.0), axis=0),
        ]
    )
    grad_gain_two = jnp.sum(back_second * normed_two, axis=0)
    grad_bias_two = jnp.sum(back_second, axis=0)
    back_residual = back_all + norm_back(back_second, normed_two, scale_two, gain_two)
    back_out = back_residual.astype(BF)
    grads_out = ring.last(grads_out, out_near, BF)
    in_near = ring.near(grads_in, in_via, BF)
    back_attended = dot(back_out, out_w).astype(BF)
    grad_out = dot_tn(back_out, attended).astype(BF)
    back_qkv = attend_back(qkv, prefix, back_attended, lse, head_dim)
    back_qkv = after(back_qkv, (in_near, grads_out))
    grads_in = ring.last(grads_in, in_near, BF)
    grad_qkv = jnp.concatenate([dot_tn(first_rows, back_qkv[i]).astype(BF) for i in range(3)], axis=1)
    first_terms = sum(dot_nt(back_qkv[i], qkv_w[:, i * part : (i + 1) * part]) for i in range(3))
    first_terms = first_terms.astype(BF)
    own_terms = lax.dynamic_slice_in_dim(first_terms, first_own, own_rows)
    other_terms = lax.dynamic_slice_in_dim(first_terms, own_rows - first_own, own_rows)
    back_first = own_terms.astype(F32) + swap(other_terms).astype(F32)

    def mine(value):
        return lax.dynamic_slice_in_dim(value, first_own, own_rows)

    normed_own = mine(normed_one)
    back_norm_one = norm_back(back_first, normed_own, mine(scale_one), gain_one)
    grad_tokens = dot_nt(
        (mine(back_residual) + back_norm_one).astype(BF), to_order
    ).astype(BF)
    one_part = jnp.stack([jnp.sum(back_first * normed_own, axis=0), jnp.sum(back_first, axis=0)])
    one_part = one_part + swap(one_part)
    small = jnp.concatenate(
        [one_part, grad_gain_two[None], grad_bias_two[None], grad_centre], axis=0
    )
    small = small.reshape(small_count, count, rows).transpose(1, 0, 2)
    grad_first = jnp.concatenate([grad_qkv, grad_out], axis=1)
    if count == 16:
        small = jnp.pad(small, ((0, 0), (0, 8 - small_count), (0, 128 - rows)))
        small, grad_first = scatter_last(small, grad_first.reshape(count, rows, 4 * part))
        small = small[:small_count, :rows]
    else:
        grad_first = ring.scatter(grad_first, BF)
        small = ring.scatter(small.reshape(count, small_count * rows), F32).reshape(small_count, rows)
    grad_qkv, grad_out = grad_first[:, : 3 * part], grad_first[:, 3 * part :]
    small = lax.dynamic_slice_in_dim(small, side * (rows // 2), rows // 2, axis=1)
    return (
        block_out,
        grad_tokens,
        small[0],
        small[1],
        grad_qkv[:, :part],
        grad_qkv[:, part : 2 * part],
        grad_qkv[:, 2 * part :],
        grad_out.T,
        small[2],
        small[3],
        small[4:],
        grads_in.reshape(rows, experts, hidden).transpose(1, 0, 2),
        grads_out.reshape(rows, experts, hidden).transpose(1, 2, 0),
    )


def solution(mesh):
    ring = Ring(mesh.shape["dp"])
    both, rows = P(("dp", "tensor")), P(("dp", "tensor"), None)
    columns = P("dp", "tensor")

    def step(*arguments):
        return body(ring, *arguments)

    return jax.shard_map(
        step,
        mesh=mesh,
        in_specs=(
            rows,
            rows,
            P("dp"),
            P("dp", None),
            both,
            both,
            columns,
            columns,
            columns,
            P("tensor", "dp"),
            both,
            both,
            P(None, ("dp", "tensor")),
            P(None, "dp", "tensor"),
            P(None, "tensor", "dp"),
        ),
        out_specs=(
            rows,
            rows,
            both,
            both,
            columns,
            columns,
            columns,
            P("tensor", "dp"),
            both,
            both,
            P(None, ("dp", "tensor")),
            P(None, "dp", "tensor"),
            P(None, "tensor", "dp"),
        ),
        check_vma=False,
    )
```

profile of v0, /device:TPU:0, one launch (start us, length us, event | category | flops | bytes accessed | tf_op | source)
XLA Modules:
  0.0 443.2 jit_solution(13955486208348050537)
XLA Ops:
  5.5 33.8 %gather_first.1 = (f32[16,8,128]{2,1,0:T(8,128)}, bf16[16,48,1536]{2,1,0:T(8,128)(2,1)}, f32[16,8,128]{2,1,0:T(8,128)}) custom-call(f32[8,128]{1,0:T(8,128)} %pad.8.vec_ref, bf16[48,1536]{1,0:T(8,128)(2,1)} %pad_maximum_fusion.10.qkv_ref), custom_call_target="tpu_custom_call" | custom-call | tf_op jit(solution)/shard_map/gather_first/pallas_call | solution.py:243
  64.1 3.4 collective-permute-done.1
  79.4 29.3 %collective-permute-done.14 = bf16[48,1536]{1,0:T(8,128)(2,1)S(1)} collective-permute-done((bf16[48,1536]{1,0:T(8,128)(2,1)S(1)}, bf16[48,1536]{1,0:T(8,128)(2,1)S(1)}, u32[]{:S(2)}, u32[]{:S(2)}) %collective-permute-start.14) | collective-permute-done | bytes 147488 | tf_op jit(solution)/shard_map/ppermute | solution.py:56
  118.8 3.7 convolution_convert_fusion.q_ref.k_ref.v_ref
  123.0 4.0 fusion.51
  127.6 17.6 %attend.1 = (bf16[1024,384]{1,0:T(8,128)(2,1)}, f32[3,8,1024]{2,1,0:T(8,128)}) custom-call(s32[1]{0:T(128)S(6)} %copy.70.prefix_ref, bf16[1024,1152]{1,0:T(8,128)(2,1)} %convolution_convert_fusion.q_ref.k_ref.v_ref, bf16[1024,1152]{1,0:T(8,128)(2,1)} %convolution_convert_fusion.q_ref.k_ref.v_ref, bf16[1024,1152]{1,0:T(8,128)(2,1)} %convolution_convert_fusion.q_ref.k_ref.v_ref), custom_call_target="tpu_custom_call" | custom-call | flops 1610612736 | bytes 3145728 | tf_op jit(solution)/shard_map/attend/pallas_call | solution.py:464
  154.1 12.7 %collective-permute-done.12 = bf16[96,3072]{1,0:T(8,128)(2,1)S(1)} collective-permute-done((bf16[96,3072]{1,0:T(8,128)(2,1)S(1)}, bf16[96,3072]{1,0:T(8,128)(2,1)S(1)}, u32[]{:S(2)}, u32[]{:S(2)}) %collective-permute-start.12) | collective-permute-done | bytes 589856 | tf_op jit(solution)/shard_map/ppermute | solution.py:56
  177.7 4.3 multiply_convert_fusion.1
  196.2 17.2 %collective-permute-done.19 = bf16[96,1536]{1,0:T(8,128)(2,1)S(1)} collective-permute-done((bf16[96,1536]{1,0:T(8,128)(2,1)S(1)}, bf16[96,1536]{1,0:T(8,128)(2,1)S(1)}, u32[]{:S(2)}, u32[]{:S(2)}) %collective-permute-start.19) | collective-permute-done | bytes 294944 | tf_op jit(solution)/shard_map/ppermute | solution.py:56
  215.2 5.7 %fusion.10 = bf16[640,1536]{1,0:T(8,128)(2,1)S(1)} fusion(f32[640,1536]{1,0:T(8,128)} %get-tuple-element.125, bf16[768,1536]{1,0:T(8,128)(2,1)S(1)} %constant_dynamic-update-slice_fusion.10, bf16[1024,768]{1,0:T(8,128)(2,1)S(1)} %fusion.55, pred[640]{0:T(1024)(128)(4,1)S(1)} %copy-done.48), kind=kOutput, calls=%fused_computation.40 | convolution fusion | flops 1530101760 | bytes 9241600 | tf_op jit(solution)/shard_map/dot_general | solution.py:365
  224.8 4.1 fusion.17
  245.5 29.3 %collective-permute-done.30 = bf16[96,3072]{1,0:T(8,128)(2,1)S(1)} collective-permute-done((bf16[96,3072]{1,0:T(8,128)(2,1)S(1)}, bf16[96,3072]{1,0:T(8,128)(2,1)S(1)}, u32[]{:S(2)}, u32[]{:S(2)}) %collective-permute-start.30) | collective-permute-done | bytes 589856 | tf_op jit(solution)/shard_map/ppermute | solution.py:56
  284.3 4.7 %collective-permute-done.34 = bf16[48,3072]{1,0:T(8,128)(2,1)S(1)} collective-permute-done((bf16[48,3072]{1,0:T(8,128)(2,1)S(1)}, bf16[48,3072]{1,0:T(8,128)(2,1)S(1)}, u32[]{:S(2)}, u32[]{:S(2)}) %collective-permute-start.34) | collective-permute-done | bytes 294944 | tf_op jit(solution)/shard_map/ppermute | solution.py:56
  290.5 6.9 %collective-permute-done.36 = bf16[48,3072]{1,0:T(8,128)(2,1)S(1)} collective-permute-done((bf16[48,3072]{1,0:T(8,128)(2,1)S(1)}, bf16[48,3072]{1,0:T(8,128)(2,1)S(1)}, u32[]{:S(2)}, u32[]{:S(2)}) %collective-permute-start.36) | collective-permute-done | bytes 294944 | tf_op jit(solution)/shard_map/ppermute | solution.py:56
  298.9 4.4 collective-permute-done.35
  304.3 4.2 fusion.25
  314.4 3.9 convert_add_fusion
  323.9 21.2 %attend_back.1 = bf16[3,1024,384]{2,1,0:T(8,128)(2,1)} custom-call(s32[1]{0:T(128)S(6)} %copy.70.prefix_ref, bf16[1024,1152]{1,0:T(8,128)(2,1)} %convolution_convert_fusion.q_ref.k_ref.v_ref, bf16[1024,1152]{1,0:T(8,128)(2,1)} %convolution_convert_fusion.q_ref.k_ref.v_ref, bf16[1024,1152]{1,0:T(8,128)(2,1)} %convolution_convert_fusion.q_ref.k_ref.v_ref, ...), custom_call_target="tpu_custom_call" | custom-call | flops 4026531840 | bytes 5505024 | tf_op jit(solution)/shard_map/attend_back/pallas_call | solution.py:485
  353.9 3.7 fusion.191
  358.3 7.4 %collective-permute-start.39 = (bf16[48,3072]{1,0:T(8,128)(2,1)}, bf16[48,3072]{1,0:T(8,128)(2,1)}, u32[]{:S(2)}, u32[]{:S(2)}) collective-permute-start(bf16[48,3072]{1,0:T(8,128)(2,1)} %get-tuple-element.100), channel_id=1, source_target_pairs={{0,16},{2,18},{4,20},{6,22},{8,0},{10,2},{12,4},{14,6},{16,24},{18... | collective-permute-start | bytes 884744 | tf_op jit(solution)/shard_map/ppermute | solution.py:56
  373.5 8.5 %collective-permute-done.41 = bf16[48,3072]{1,0:T(8,128)(2,1)} collective-permute-done((bf16[48,3072]{1,0:T(8,128)(2,1)S(1)}, bf16[48,3072]{1,0:T(8,128)(2,1)}, u32[]{:S(2)}, u32[]{:S(2)}) %collective-permute-start.41) | collective-permute-done | bytes 294944 | tf_op jit(solution)/shard_map/ppermute | solution.py:56
  382.0 5.5 %collective-permute-done.40 = bf16[48,3072]{1,0:T(8,128)(2,1)} collective-permute-done((bf16[48,3072]{1,0:T(8,128)(2,1)S(1)}, bf16[48,3072]{1,0:T(8,128)(2,1)}, u32[]{:S(2)}, u32[]{:S(2)}) %collective-permute-start.40) | collective-permute-done | bytes 294944 | tf_op jit(solution)/shard_map/ppermute | solution.py:56
  392.6 3.7 fusion.90
  397.1 42.3 %scatter_last.1 = (f32[8,128]{1,0:T(8,128)}, f32[48,1536]{1,0:T(8,128)}) custom-call(f32[16,8,128]{2,1,0:T(8,128)} %pad.9.small_ref, bf16[16,48,1536]{2,1,0:T(8,128)(2,1)} %bitcast.96), custom_call_target="tpu_custom_call" | custom-call | tf_op jit(solution)/shard_map/scatter_last/pallas_call | solution.py:341
  (314 shorter events, 158.1 us)
Async XLA Ops:
  40.8 23.3 %collective-permute-start.3 = (bf16[48,3072]{1,0:T(8,128)(2,1)S(1)}, bf16[48,3072]{1,0:T(8,128)(2,1)S(1)}, u32[]{:S(2)}, u32[]{:S(2)}) collective-permute-start(bf16[48,3072]{1,0:T(8,128)(2,1)S(1)} %bitcast.107), channel_id=1, source_target_pairs={{0,16},{2,18},{4,20},{6,22},{8,0},{10,2},{12,4},{14,6},{16,24},{18... | collective-permute-start | bytes 884744 | tf_op jit(solution)/shard_map/ppermute | solution.py:56
  43.8 23.7 %collective-permute-start.1 = (bf16[48,3072]{1,0:T(8,128)(2,1)S(1)}, bf16[48,3072]{1,0:T(8,128)(2,1)S(1)}, u32[]{:S(2)}, u32[]{:S(2)}) collective-permute-start(bf16[48,3072]{1,0:T(8,128)(2,1)S(1)} %bitcast.109), channel_id=1, source_target_pairs={{0,8},{2,10},{4,12},{6,14},{8,24},{10,26},{12,28},{14,30},{16,0},{... | collective-permute-start | bytes 884744 | tf_op jit(solution)/shard_map/ppermute | solution.py:56
  53.7 57.5 %collective-permute-start = (bf16[512,768]{1,0:T(8,128)(2,1)}, bf16[512,768]{1,0:T(8,128)(2,1)S(1)}, u32[]{:S(2)}, u32[]{:S(2)}) collective-permute-start(bf16[512,768]{1,0:T(8,128)(2,1)} %param.15), channel_id=1, source_target_pairs={{0,1},{1,0},{2,3},{3,2},{4,5},{5,4},{6,7},{7,6},{8,9},{9,8},{10,11... | collective-permute-start | bytes 2359304 | tf_op jit(solution)/shard_map/ppermute | solution.py:357
  63.4 59.1 %collective-permute-start.9 = (bf16[512,768]{1,0:T(8,128)(2,1)}, bf16[512,768]{1,0:T(8,128)(2,1)S(1)}, u32[]{:S(2)}, u32[]{:S(2)}) collective-permute-start(bf16[512,768]{1,0:T(8,128)(2,1)} %param.16), channel_id=1, source_target_pairs={{0,1},{1,0},{2,3},{3,2},{4,5},{5,4},{6,7},{7,6},{8,9},{9,8},{10,11... | collective-permute-start | bytes 2359304 | tf_op jit(solution)/shard_map/ppermute | solution.py:357
  69.9 38.8 %collective-permute-start.14 = (bf16[48,1536]{1,0:T(8,128)(2,1)S(1)}, bf16[48,1536]{1,0:T(8,128)(2,1)S(1)}, u32[]{:S(2)}, u32[]{:S(2)}) collective-permute-start(bf16[48,1536]{1,0:T(8,128)(2,1)S(1)} %get-tuple-element.45), channel_id=1, source_target_pairs={{0,8},{2,10},{4,12},{6,14},{8,24},{10,26},{12,28},{14,30},{16,0},{... | collective-permute-start | bytes 442376 | tf_op jit(solution)/shard_map/ppermute | solution.py:56
  73.5 74.0 %collective-permute-start.23 = (bf16[192,1536]{1,0:T(8,128)(2,1)}, bf16[192,1536]{1,0:T(8,128)(2,1)}, u32[]{:S(2)}, u32[]{:S(2)}) collective-permute-start(bf16[192,1536]{1,0:T(8,128)(2,1)} %constant_dynamic-update-slice_fusion), channel_id=1, source_target_pairs={{0,16},{2,18},{4,20},{6,22},{8,0},{10,2},{12,4},{14,6},{16,24},{18... | collective-permute-start | bytes 1769480 | tf_op jit(solution)/shard_map/ppermute | solution.py:56
  77.7 69.9 %collective-permute-start.22 = (bf16[192,1536]{1,0:T(8,128)(2,1)}, bf16[192,1536]{1,0:T(8,128)(2,1)}, u32[]{:S(2)}, u32[]{:S(2)}) collective-permute-start(bf16[192,1536]{1,0:T(8,128)(2,1)} %constant_dynamic-update-slice_fusion), channel_id=1, source_target_pairs={{0,24},{2,26},{4,28},{6,30},{8,16},{10,18},{12,20},{14,22},{16,8},... | collective-permute-start | bytes 1769480 | tf_op jit(solution)/shard_map/ppermute | solution.py:56
  108.7 40.9 %collective-permute-start.11 = (bf16[192,3072]{1,0:T(8,128)(2,1)S(1)}, bf16[192,3072]{1,0:T(8,128)(2,1)S(1)}, u32[]{:S(2)}, u32[]{:S(2)}) collective-permute-start(bf16[192,3072]{1,0:T(8,128)(2,1)S(1)} %pad_maximum_fusion.3), channel_id=1, source_target_pairs={{0,2},{2,0},{4,6},{6,4},{8,10},{10,8},{12,14},{14,12},{16,18},{18,... | collective-permute-start | bytes 3538952 | tf_op jit(solution)/shard_map/ppermute | solution.py:56
  111.3 40.0 %collective-permute-start.10 = (bf16[192,3072]{1,0:T(8,128)(2,1)S(1)}, bf16[192,3072]{1,0:T(8,128)(2,1)S(1)}, u32[]{:S(2)}, u32[]{:S(2)}) collective-permute-start(bf16[192,3072]{1,0:T(8,128)(2,1)S(1)} %pad_maximum_fusion.3), channel_id=1, source_target_pairs={{0,4},{2,6},{4,0},{6,2},{8,12},{10,14},{12,8},{14,10},{16,20},{18,... | collective-permute-start | bytes 3538952 | tf_op jit(solution)/shard_map/ppermute | solution.py:56
  122.5 25.2 %collective-permute-start.21 = (bf16[192,1536]{1,0:T(8,128)(2,1)}, bf16[192,1536]{1,0:T(8,128)(2,1)}, u32[]{:S(2)}, u32[]{:S(2)}) collective-permute-start(bf16[192,1536]{1,0:T(8,128)(2,1)} %constant_dynamic-update-slice_fusion), channel_id=1, source_target_pairs={{0,8},{2,10},{4,12},{6,14},{8,24},{10,26},{12,28},{14,30},{16,0},{... | collective-permute-start | bytes 1769480 | tf_op jit(solution)/shard_map/ppermute | solution.py:56
  147.6 22.0 %collective-permute-start.8 = (bf16[1024,768]{0,1:T(8,128)(2,1)S(1)}, bf16[1024,768]{0,1:T(8,128)(2,1)S(1)}, u32[]{:S(2)}, u32[]{:S(2)}) collective-permute-start(bf16[1024,768]{0,1:T(8,128)(2,1)S(1)} %convolution_convert_fusion.5), channel_id=1, source_target_pairs={{0,1},{1,0},{2,3},{3,2},{4,5},{5,4},{6,7},{7,6},{8,9},{9,8},{10,11... | collective-permute-start | bytes 4718600 | tf_op jit(solution)/shard_map/ppermute | solution.py:357
  168.6 26.3 %collective-permute-start.18 = (bf16[192,1536]{1,0:T(8,128)(2,1)S(1)}, bf16[192,1536]{1,0:T(8,128)(2,1)S(1)}, u32[]{:S(2)}, u32[]{:S(2)}) collective-permute-start(bf16[192,1536]{1,0:T(8,128)(2,1)S(1)} %copy-done.17), channel_id=1, source_target_pairs={{0,2},{2,0},{4,6},{6,4},{8,10},{10,8},{12,14},{14,12},{16,18},{18,... | collective-permute-start | bytes 1769480 | tf_op jit(solution)/shard_map/ppermute | solution.py:56
  169.1 26.4 %collective-permute-start.17 = (bf16[192,1536]{1,0:T(8,128)(2,1)S(1)}, bf16[192,1536]{1,0:T(8,128)(2,1)S(1)}, u32[]{:S(2)}, u32[]{:S(2)}) collective-permute-start(bf16[192,1536]{1,0:T(8,128)(2,1)S(1)} %copy-done.17), channel_id=1, source_target_pairs={{0,4},{2,6},{4,0},{6,2},{8,12},{10,14},{12,8},{14,10},{16,20},{18,... | collective-permute-start | bytes 1769480 | tf_op jit(solution)/shard_map/ppermute | solution.py:56
  191.8 33.0 %collective-permute-start.26 = (bf16[96,3072]{1,0:T(8,128)(2,1)S(1)}, bf16[96,3072]{1,0:T(8,128)(2,1)S(1)}, u32[]{:S(2)}, u32[]{:S(2)}) collective-permute-start(bf16[96,3072]{1,0:T(8,128)(2,1)S(1)} %get-tuple-element.88), channel_id=1, source_target_pairs={{0,4},{2,6},{4,0},{6,2},{8,12},{10,14},{12,8},{14,10},{16,20},{18,... | collective-permute-start | bytes 1769480 | tf_op jit(solution)/shard_map/ppermute | solution.py:56
  193.4 31.4 %collective-permute-start.25 = (bf16[96,3072]{1,0:T(8,128)(2,1)S(1)}, bf16[96,3072]{1,0:T(8,128)(2,1)S(1)}, u32[]{:S(2)}, u32[]{:S(2)}) collective-permute-start(bf16[96,3072]{1,0:T(8,128)(2,1)S(1)} %get-tuple-element.89), channel_id=1, source_target_pairs={{0,2},{2,0},{4,6},{6,4},{8,10},{10,8},{12,14},{14,12},{16,18},{18,... | collective-permute-start | bytes 1769480 | tf_op jit(solution)/shard_map/ppermute | solution.py:56
  235.0 41.3 %collective-permute-start.33 = (bf16[192,3072]{1,0:T(8,128)(2,1)}, bf16[192,3072]{1,0:T(8,128)(2,1)}, u32[]{:S(2)}, u32[]{:S(2)}) collective-permute-start(bf16[192,3072]{1,0:T(8,128)(2,1)} %fusion.95), channel_id=1, source_target_pairs={{0,4},{2,6},{4,0},{6,2},{8,12},{10,14},{12,8},{14,10},{16,20},{18,... | collective-permute-start | bytes 3538952 | tf_op jit(solution)/shard_map/ppermute | solution.py:56
  236.7 39.6 %collective-permute-start.32 = (bf16[192,3072]{1,0:T(8,128)(2,1)}, bf16[192,3072]{1,0:T(8,128)(2,1)}, u32[]{:S(2)}, u32[]{:S(2)}) collective-permute-start(bf16[192,3072]{1,0:T(8,128)(2,1)} %pad_maximum_fusion.6), channel_id=1, source_target_pairs={{0,2},{2,0},{4,6},{6,4},{8,10},{10,8},{12,14},{14,12},{16,18},{18,... | collective-permute-start | bytes 3538952 | tf_op jit(solution)/shard_map/ppermute | solution.py:56
  240.3 64.0 %collective-permute-start.24 = (bf16[1024,768]{0,1:T(8,128)(2,1)S(1)}, bf16[1024,768]{0,1:T(8,128)(2,1)}, u32[]{:S(2)}, u32[]{:S(2)}) collective-permute-start(bf16[1024,768]{0,1:T(8,128)(2,1)S(1)} %fusion.58), channel_id=1, source_target_pairs={{0,1},{1,0},{2,3},{3,2},{4,5},{5,4},{6,7},{7,6},{8,9},{9,8},{10,11... | collective-permute-start | bytes 4718600 | tf_op jit(solution)/shard_map/ppermute | solution.py:357
  241.2 33.7 %collective-permute-start.30 = (bf16[96,3072]{1,0:T(8,128)(2,1)S(1)}, bf16[96,3072]{1,0:T(8,128)(2,1)S(1)}, u32[]{:S(2)}, u32[]{:S(2)}) collective-permute-start(bf16[96,3072]{1,0:T(8,128)(2,1)S(1)} %get-tuple-element.94), channel_id=1, source_target_pairs={{0,2},{2,0},{4,6},{6,4},{8,10},{10,8},{12,14},{14,12},{16,18},{18,... | collective-permute-start | bytes 1769480 | tf_op jit(solution)/shard_map/ppermute | solution.py:56
  241.8 33.1 %collective-permute-start.28 = (bf16[96,3072]{1,0:T(8,128)(2,1)S(1)}, bf16[96,3072]{1,0:T(8,128)(2,1)S(1)}, u32[]{:S(2)}, u32[]{:S(2)}) collective-permute-start(bf16[96,3072]{1,0:T(8,128)(2,1)S(1)} %get-tuple-element.95), channel_id=1, source_target_pairs={{0,4},{2,6},{4,0},{6,2},{8,12},{10,14},{12,8},{14,10},{16,20},{18,... | collective-permute-start | bytes 1769480 | tf_op jit(solution)/shard_map/ppermute | solution.py:56
  274.8 33.7 %collective-permute-start.27 = (bf16[1024,768]{0,1:T(8,128)(2,1)S(1)}, bf16[1024,768]{0,1:T(8,128)(2,1)S(1)}, u32[]{:S(2)}, u32[]{:S(2)}) collective-permute-start(bf16[1024,768]{0,1:T(8,128)(2,1)S(1)} %fusion.59), channel_id=1, source_target_pairs={{0,1},{1,0},{2,3},{3,2},{4,5},{5,4},{6,7},{7,6},{8,9},{9,8},{10,11... | collective-permute-start | bytes 4718600 | tf_op jit(solution)/shard_map/ppermute | solution.py:357
  281.5 21.8 %collective-permute-start.35 = (bf16[48,3072]{1,0:T(8,128)(2,1)S(1)}, bf16[48,3072]{1,0:T(8,128)(2,1)S(1)}, u32[]{:S(2)}, u32[]{:S(2)}) collective-permute-start(bf16[48,3072]{1,0:T(8,128)(2,1)S(1)} %get-tuple-element.105), channel_id=1, source_target_pairs={{0,24},{2,26},{4,28},{6,30},{8,16},{10,18},{12,20},{14,22},{16,8},... | collective-permute-start | bytes 884744 | tf_op jit(solution)/shard_map/ppermute | solution.py:56
  288.9 56.2 %collective-permute-start.29 = (bf16[192,3072]{1,0:T(8,128)(2,1)}, bf16[192,3072]{1,0:T(8,128)(2,1)}, u32[]{:S(2)}, u32[]{:S(2)}) collective-permute-start(bf16[192,3072]{1,0:T(8,128)(2,1)} %pad_maximum_fusion.4), channel_id=1, source_target_pairs={{0,2},{2,0},{4,6},{6,4},{8,10},{10,8},{12,14},{14,12},{16,18},{18,... | collective-permute-start | bytes 3538952 | tf_op jit(solution)/shard_map/ppermute | solution.py:56
  297.4 47.7 %collective-permute-start.31 = (bf16[192,3072]{1,0:T(8,128)(2,1)}, bf16[192,3072]{1,0:T(8,128)(2,1)}, u32[]{:S(2)}, u32[]{:S(2)}) collective-permute-start(bf16[192,3072]{1,0:T(8,128)(2,1)} %pad_maximum_fusion.5), channel_id=1, source_target_pairs={{0,4},{2,6},{4,0},{6,2},{8,12},{10,14},{12,8},{14,10},{16,20},{18,... | collective-permute-start | bytes 3538952 | tf_op jit(solution)/shard_map/ppermute | solution.py:56
  (74 other events, 959.8 us)
where the time goes:
time: 450 us; the launch traced here: 443 us
  waiting for transfers between devices  133 us (30%)
  Pallas kernels  115 us (26%)
  matrix products  71.5 us (16%)
  starting transfers between devices  45.1 us (10%)
  other arithmetic  40 us (9%)
  local copies, waits for them, and re-layouts  35.7 us (8%)
    ppermute x35, waiting for transfers between devices, move(): return lax.ppermute(value, 'dp', self.shift(stage, step))  133 us
    ppermute x35, starting transfers between devices, move(): return lax.ppermute(value, 'dp', self.shift(stage, step))  44.9 us
    pallas_call x1, Pallas kernels, scatter_last(): pl.pallas_call(scatter_kernel, out_shape=(jax.ShapeDtypeStruct(small.shap...  42.3 us
    dot_general x11, matrix products, dot(): lax.dot_general(a, b, (((1,), (0,)), ((), ())), preferred_element_type=F32)  34.4 us
    pallas_call x1, Pallas kernels, gather_first(): pl.pallas_call(gather_kernel, out_shape=(jax.ShapeDtypeStruct((16, *vecto...  33.8 us
    pallas_call x1, Pallas kernels, attend_back(): pl.pallas_call(functools.partial(attend_back_kernel, head_dim), grid=(gro...  21.2 us
    dot_general x10, matrix products, dot_tn(): lax.dot_general(a, b, (((0,), (0,)), ((), ())), preferred_element_type=F32)  19.3 us
    dot_general x10, matrix products, dot_nt(): lax.dot_general(a, b, (((1,), (1,)), ((), ())), preferred_element_type=F32)  17.9 us
  transfers between devices with their start and end apart: 42, of which 15 were waited for; matrix products, arithmetic and copies ran while one was open for 24% of the time, Pallas kernels for 9%

commit v1 on v0

--- a/solution.py
+++ b/solution.py
@@ -567,18 +567,24 @@
     gain_one, bias_one, gain_two, bias_two = (table[i : i + 1] for i in range(4))
     centres = table[4:]
 
-    qkv_w, in_block, turned_block = lax.optimization_barrier((qkv_w, in_block, turned_block))
+    qkv_w, in_block, out_block, turned_block = lax.optimization_barrier(
+        (qkv_w, in_block, out_block, turned_block)
+    )
     qkv_w, out_w = qkv_w[:, : 3 * part], qkv_w[:, 3 * part :]
-    in_lead = ring.lead(in_block)
     if count == 16:
+        joint = jnp.concatenate([in_block, out_block], axis=1)
+        leads = [joint] + [ring.move(joint, 0, step) for step in range(1, 4)]
+        wide = in_block.shape[1]
+        in_lead = jnp.concatenate([lead[:, :wide] for lead in leads], axis=0)
+        out_lead = jnp.concatenate([lead[:, wide:] for lead in leads], axis=0)
         turned_crossed = ring.cross(turned_block)
         turned_square = ring.close(turned_block, turned_crossed)
-        in_lead, turned_square = lax.optimization_barrier((in_lead, turned_square))
+        in_lead, out_lead, turned_square = lax.optimization_barrier((in_lead, out_lead, turned_square))
         turned_w = ring.along(turned_square)
     else:
+        in_lead, out_lead = ring.lead(in_block), ring.lead(out_block)
         turned_w = ring.gather(turned_block)
     in_crossed = ring.cross(in_lead)
-    out_lead = ring.lead(after(out_block, in_lead))
     in_w = ring.close(in_lead, in_crossed)
     out_crossed = ring.cross(after(out_lead, in_w))
     back_ws = (ring.close(out_lead, out_crossed), turned_w)

time: 450 us -> 414 us (0.920)
  waiting for transfers between devices: 133 us -> 104 us
  starting transfers between devices: 45.1 us -> 39.4 us
    ppermute x35 -> x32, waiting for transfers between devices: 133 us -> 104 us  [move(): return lax.ppermute(value, 'dp', self.shift(stage, step))]
    ppermute x35 -> x32, starting transfers between devices: 44.9 us -> 39.2 us  [move(): return lax.ppermute(value, 'dp', self.shift(stage, step))]
    unnamed x116 -> x117, local copies, waits for them, and re-layouts: 13.2 us -> 12.5 us
  transfers between devices with their start and end apart: 42 -> 39, of which waited for: 15 -> 13; matrix products, arithmetic and copies ran while one was open for 24% -> 29% of each run, Pallas kernels for 9% -> 10%
where the time goes in v1:
time: 414 us; the launch traced here: 407 us
  Pallas kernels  114 us (28%)
  waiting for transfers between devices  104 us (25%)
  matrix products  70.9 us (17%)
  other arithmetic  39.7 us (10%)
  starting transfers between devices  39.4 us (10%)
  local copies, waits for them, and re-layouts  35.8 us (9%)
    ppermute x32, waiting for transfers between devices, move(): return lax.ppermute(value, 'dp', self.shift(stage, step))  104 us
    pallas_call x1, Pallas kernels, scatter_last(): pl.pallas_call(scatter_kernel, out_shape=(jax.ShapeDtypeStruct(small.shap...  41.5 us
    ppermute x32, starting transfers between devices, move(): return lax.ppermute(value, 'dp', self.shift(stage, step))  39.2 us
    pallas_call x1, Pallas kernels, gather_first(): pl.pallas_call(gather_kernel, out_shape=(jax.ShapeDtypeStruct((16, *vecto...  33.8 us
    dot_general x11, matrix products, dot(): lax.dot_general(a, b, (((1,), (0,)), ((), ())), preferred_element_type=F32)  33.7 us
    pallas_call x1, Pallas kernels, attend_back(): pl.pallas_call(functools.partial(attend_back_kernel, head_dim), grid=(gro...  21.2 us
    dot_general x10, matrix products, dot_tn(): lax.dot_general(a, b, (((0,), (0,)), ((), ())), preferred_element_type=F32)  19 us
    dot_general x10, matrix products, dot_nt(): lax.dot_general(a, b, (((1,), (1,)), ((), ())), preferred_element_type=F32)  18.1 us
  transfers between devices with their start and end apart: 39, of which 13 were waited for; matrix products, arithmetic and copies ran while one was open for 29% of the time, Pallas kernels for 10%

profile of v1, /device:TPU:0, one launch (start us, length us, event | category | flops | bytes accessed | tf_op | source)
XLA Modules:
  0.0 407.5 jit_solution(7572766639095406000)
XLA Ops:
  5.5 33.8 %gather_first.1 = (f32[16,8,128]{2,1,0:T(8,128)}, bf16[16,48,1536]{2,1,0:T(8,128)(2,1)}, f32[16,8,128]{2,1,0:T(8,128)}) custom-call(f32[8,128]{1,0:T(8,128)} %pad.8.vec_ref, bf16[48,1536]{1,0:T(8,128)(2,1)} %pad_maximum_fusion.10.qkv_ref), custom_call_target="tpu_custom_call" | custom-call | tf_op jit(solution)/shard_map/gather_first/pallas_call | solution.py:243
  54.9 2.9 collective-permute-done.6
  64.4 15.8 %collective-permute-done.1 = bf16[48,4608]{1,0:T(8,128)(2,1)S(1)} collective-permute-done((bf16[48,4608]{1,0:T(8,128)(2,1)S(1)}, bf16[48,4608]{1,0:T(8,128)(2,1)S(1)}, u32[]{:S(2)}, u32[]{:S(2)}) %collective-permute-start.1) | collective-permute-done | bytes 442400 | tf_op jit(solution)/shard_map/ppermute | solution.py:56
  92.3 3.7 convolution_convert_fusion.q_ref.k_ref.v_ref
  100.8 17.6 %attend.1 = (bf16[1024,384]{1,0:T(8,128)(2,1)}, f32[3,8,1024]{2,1,0:T(8,128)}) custom-call(s32[1]{0:T(128)S(6)} %copy.72.prefix_ref, bf16[1024,1152]{1,0:T(8,128)(2,1)} %convolution_convert_fusion.q_ref.k_ref.v_ref, bf16[1024,1152]{1,0:T(8,128)(2,1)} %convolution_convert_fusion.q_ref.k_ref.v_ref, bf16[1024,1152]{1,0:T(8,128)(2,1)} %convolution_convert_fusion.q_ref.k_ref.v_ref), custom_call_target="tpu_custom_call" | custom-call | flops 1610612736 | bytes 3145728 | tf_op jit(solution)/shard_map/attend/pallas_call | solution.py:464
  120.9 13.6 %collective-permute-done.18 = bf16[192,1536]{1,0:T(8,128)(2,1)} collective-permute-done((bf16[192,1536]{1,0:T(8,128)(2,1)}, bf16[192,1536]{1,0:T(8,128)(2,1)}, u32[]{:S(2)}, u32[]{:S(2)}) %collective-permute-start.18) | collective-permute-done | bytes 589856 | tf_op jit(solution)/shard_map/ppermute | solution.py:56
  140.8 11.2 %collective-permute-done.12 = bf16[96,3072]{1,0:T(8,128)(2,1)S(1)} collective-permute-done((bf16[96,3072]{1,0:T(8,128)(2,1)S(1)}, bf16[96,3072]{1,0:T(8,128)(2,1)S(1)}, u32[]{:S(2)}, u32[]{:S(2)}) %collective-permute-start.12) | collective-permute-done | bytes 589856 | tf_op jit(solution)/shard_map/ppermute | solution.py:56
  162.6 4.2 %multiply_convert_fusion = (bf16[640,1536]{1,0:T(8,128)(2,1)S(1)}, f32[640,1536]{1,0:T(8,128)}) fusion(bf16[768,3072]{1,0:T(8,128)(2,1)S(1)} %bitcast.112, bf16[1024,768]{1,0:T(8,128)(2,1)S(1)} %fusion.52), kind=kOutput, calls=%fused_computation.48 | convolution fusion | flops 1518796800 | bytes 9240576 | tf_op jit(solution)/shard_map/dot_general | solution.py:365
  166.8 4.2 %multiply_convert_fusion.1 = (bf16[640,1536]{1,0:T(8,128)(2,1)S(1)}, f32[640,1536]{1,0:T(8,128)}) fusion(bf16[768,3072]{1,0:T(8,128)(2,1)S(1)} %bitcast.112, bf16[1024,768]{1,0:T(8,128)(2,1)S(1)} %fusion.52), kind=kOutput, calls=%fused_computation.49 | convolution fusion | flops 1518796800 | bytes 9240576 | tf_op jit(solution)/shard_map/dot_general | solution.py:365
  184.7 9.2 %collective-permute-done.23 = bf16[96,3072]{1,0:T(8,128)(2,1)S(1)} collective-permute-done((bf16[96,3072]{1,0:T(8,128)(2,1)S(1)}, bf16[96,3072]{1,0:T(8,128)(2,1)S(1)}, u32[]{:S(2)}, u32[]{:S(2)}) %collective-permute-start.23) | collective-permute-done | bytes 589856 | tf_op jit(solution)/shard_map/ppermute | solution.py:56
  194.4 5.2 %fusion.17 = bf16[640,1536]{1,0:T(8,128)(2,1)S(1)} fusion(f32[640,1536]{1,0:T(8,128)} %get-tuple-element.125, bf16[640,768]{1,0:T(8,128)(2,1)S(1)} %slice_select_fusion, bf16[768,1536]{1,0:T(8,128)(2,1)S(1)} %bitcast.106), kind=kOutput, calls=%fused_computation.47 | convolution fusion | flops 1529610240 | bytes 9240576 | tf_op jit(solution)/shard_map/dot_general | solution.py:365
  210.3 5.8 %fusion.10 = bf16[640,1536]{1,0:T(8,128)(2,1)S(1)} fusion(f32[640,1536]{1,0:T(8,128)} %get-tuple-element.127, bf16[768,1536]{1,0:T(8,128)(2,1)S(1)} %constant_dynamic-update-slice_fusion.12, bf16[1024,768]{1,0:T(8,128)(2,1)S(1)} %fusion.55, pred[640]{0:T(1024)(128)(4,1)S(1)} %copy-done.46), kind=kOutput, calls=%fused_computation.40 | convolution fusion | flops 1530101760 | bytes 9241600 | tf_op jit(solution)/shard_map/dot_general | solution.py:365
  228.6 14.1 %collective-permute-done.27 = bf16[96,3072]{1,0:T(8,128)(2,1)S(1)} collective-permute-done((bf16[96,3072]{1,0:T(8,128)(2,1)S(1)}, bf16[96,3072]{1,0:T(8,128)(2,1)S(1)}, u32[]{:S(2)}, u32[]{:S(2)}) %collective-permute-start.27) | collective-permute-done | bytes 589856 | tf_op jit(solution)/shard_map/ppermute | solution.py:56
  251.0 17.5 %collective-permute-done.31 = bf16[48,3072]{1,0:T(8,128)(2,1)S(1)} collective-permute-done((bf16[48,3072]{1,0:T(8,128)(2,1)S(1)}, bf16[48,3072]{1,0:T(8,128)(2,1)S(1)}, u32[]{:S(2)}, u32[]{:S(2)}) %collective-permute-start.31) | collective-permute-done | bytes 294944 | tf_op jit(solution)/shard_map/ppermute | solution.py:56
  270.0 4.2 %fusion.25 = (f32[1024]{0:T(1024)S(1)}, f32[1024,768]{0,1:T(8,128)}) fusion(bf16[1024,768]{0,1:T(8,128)(2,1)S(1)} %copy-done.8, bf16[1024,768]{0,1:T(8,128)(2,1)} %collective-permute-done.21, bf16[1024,768]{0,1:T(8,128)(2,1)S(1)} %fusion.58), kind=kLoop, calls=%fused_computation.63 | loop fusion | flops 4717568 | bytes 7868416 | tf_op jit(solution)/shard_map/reduce_sum | solution.py:667
  274.3 3.0 fusion.21
  280.1 3.9 convert_add_fusion
  289.6 21.2 %attend_back.1 = bf16[3,1024,384]{2,1,0:T(8,128)(2,1)} custom-call(s32[1]{0:T(128)S(6)} %copy.72.prefix_ref, bf16[1024,1152]{1,0:T(8,128)(2,1)} %convolution_convert_fusion.q_ref.k_ref.v_ref, bf16[1024,1152]{1,0:T(8,128)(2,1)} %convolution_convert_fusion.q_ref.k_ref.v_ref, bf16[1024,1152]{1,0:T(8,128)(2,1)} %convolution_convert_fusion.q_ref.k_ref.v_ref, ...), custom_call_target="tpu_custom_call" | custom-call | flops 4026531840 | bytes 5505024 | tf_op jit(solution)/shard_map/attend_back/pallas_call | solution.py:485
  319.6 3.7 fusion.191
  324.1 7.0 %collective-permute-start.36 = (bf16[48,3072]{1,0:T(8,128)(2,1)}, bf16[48,3072]{1,0:T(8,128)(2,1)}, u32[]{:S(2)}, u32[]{:S(2)}) collective-permute-start(bf16[48,3072]{1,0:T(8,128)(2,1)} %get-tuple-element.102), channel_id=1, source_target_pairs={{0,16},{2,18},{4,20},{6,22},{8,0},{10,2},{12,4},{14,6},{16,24},{18... | collective-permute-start | bytes 884744 | tf_op jit(solution)/shard_map/ppermute | solution.py:56
  338.8 8.4 %collective-permute-done.38 = bf16[48,3072]{1,0:T(8,128)(2,1)} collective-permute-done((bf16[48,3072]{1,0:T(8,128)(2,1)S(1)}, bf16[48,3072]{1,0:T(8,128)(2,1)}, u32[]{:S(2)}, u32[]{:S(2)}) %collective-permute-start.38) | collective-permute-done | bytes 294944 | tf_op jit(solution)/shard_map/ppermute | solution.py:56
  347.1 5.5 %collective-permute-done.37 = bf16[48,3072]{1,0:T(8,128)(2,1)} collective-permute-done((bf16[48,3072]{1,0:T(8,128)(2,1)S(1)}, bf16[48,3072]{1,0:T(8,128)(2,1)}, u32[]{:S(2)}, u32[]{:S(2)}) %collective-permute-start.37) | collective-permute-done | bytes 294944 | tf_op jit(solution)/shard_map/ppermute | solution.py:56
  357.7 3.7 fusion.90
  362.2 41.5 %scatter_last.1 = (f32[8,128]{1,0:T(8,128)}, f32[48,1536]{1,0:T(8,128)}) custom-call(f32[16,8,128]{2,1,0:T(8,128)} %pad.9.small_ref, bf16[16,48,1536]{2,1,0:T(8,128)(2,1)} %bitcast.96), custom_call_target="tpu_custom_call" | custom-call | tf_op jit(solution)/shard_map/scatter_last/pallas_call | solution.py:341
  (314 shorter events, 143.1 us)
Async XLA Ops:
  40.9 21.9 %collective-permute-start.3 = (bf16[48,4608]{1,0:T(8,128)(2,1)S(1)}, bf16[48,4608]{1,0:T(8,128)(2,1)S(1)}, u32[]{:S(2)}, u32[]{:S(2)}) collective-permute-start(bf16[48,4608]{1,0:T(8,128)(2,1)S(1)} %constant_dynamic-update-slice_fusion), channel_id=1, source_target_pairs={{0,16},{2,18},{4,20},{6,22},{8,0},{10,2},{12,4},{14,6},{16,24},{18... | collective-permute-start | bytes 1327112 | tf_op jit(solution)/shard_map/ppermute | solution.py:56
  42.5 21.9 %collective-permute-start.2 = (bf16[48,4608]{1,0:T(8,128)(2,1)S(1)}, bf16[48,4608]{1,0:T(8,128)(2,1)S(1)}, u32[]{:S(2)}, u32[]{:S(2)}) collective-permute-start(bf16[48,4608]{1,0:T(8,128)(2,1)S(1)} %constant_dynamic-update-slice_fusion), channel_id=1, source_target_pairs={{0,24},{2,26},{4,28},{6,30},{8,16},{10,18},{12,20},{14,22},{16,8},... | collective-permute-start | bytes 1327112 | tf_op jit(solution)/shard_map/ppermute | solution.py:56
  43.9 36.3 %collective-permute-start.1 = (bf16[48,4608]{1,0:T(8,128)(2,1)S(1)}, bf16[48,4608]{1,0:T(8,128)(2,1)S(1)}, u32[]{:S(2)}, u32[]{:S(2)}) collective-permute-start(bf16[48,4608]{1,0:T(8,128)(2,1)S(1)} %constant_dynamic-update-slice_fusion), channel_id=1, source_target_pairs={{0,8},{2,10},{4,12},{6,14},{8,24},{10,26},{12,28},{14,30},{16,0},{... | collective-permute-start | bytes 1327112 | tf_op jit(solution)/shard_map/ppermute | solution.py:56
  52.4 33.9 %collective-permute-start = (bf16[512,768]{1,0:T(8,128)(2,1)}, bf16[512,768]{1,0:T(8,128)(2,1)S(1)}, u32[]{:S(2)}, u32[]{:S(2)}) collective-permute-start(bf16[512,768]{1,0:T(8,128)(2,1)} %param.15), channel_id=1, source_target_pairs={{0,1},{1,0},{2,3},{3,2},{4,5},{5,4},{6,7},{7,6},{8,9},{9,8},{10,11... | collective-permute-start | bytes 2359304 | tf_op jit(solution)/shard_map/ppermute | solution.py:357
  62.1 33.9 %collective-permute-start.9 = (bf16[512,768]{1,0:T(8,128)(2,1)}, bf16[512,768]{1,0:T(8,128)(2,1)S(1)}, u32[]{:S(2)}, u32[]{:S(2)}) collective-permute-start(bf16[512,768]{1,0:T(8,128)(2,1)} %param.16), channel_id=1, source_target_pairs={{0,1},{1,0},{2,3},{3,2},{4,5},{5,4},{6,7},{7,6},{8,9},{9,8},{10,11... | collective-permute-start | bytes 2359304 | tf_op jit(solution)/shard_map/ppermute | solution.py:357
  80.5 40.3 %collective-permute-start.20 = (bf16[192,1536]{1,0:T(8,128)(2,1)}, bf16[192,1536]{1,0:T(8,128)(2,1)}, u32[]{:S(2)}, u32[]{:S(2)}) collective-permute-start(bf16[192,1536]{1,0:T(8,128)(2,1)} %constant_dynamic-update-slice_fusion.2), channel_id=1, source_target_pairs={{0,16},{2,18},{4,20},{6,22},{8,0},{10,2},{12,4},{14,6},{16,24},{18... | collective-permute-start | bytes 1769480 | tf_op jit(solution)/shard_map/ppermute | solution.py:56
  80.6 40.3 %collective-permute-start.19 = (bf16[192,1536]{1,0:T(8,128)(2,1)}, bf16[192,1536]{1,0:T(8,128)(2,1)}, u32[]{:S(2)}, u32[]{:S(2)}) collective-permute-start(bf16[192,1536]{1,0:T(8,128)(2,1)} %constant_dynamic-update-slice_fusion.2), channel_id=1, source_target_pairs={{0,24},{2,26},{4,28},{6,30},{8,16},{10,18},{12,20},{14,22},{16,8},... | collective-permute-start | bytes 1769480 | tf_op jit(solution)/shard_map/ppermute | solution.py:56
  82.8 53.6 %collective-permute-start.11 = (bf16[192,3072]{1,0:T(8,128)(2,1)S(1)}, bf16[192,3072]{1,0:T(8,128)(2,1)S(1)}, u32[]{:S(2)}, u32[]{:S(2)}) collective-permute-start(bf16[192,3072]{1,0:T(8,128)(2,1)S(1)} %pad_maximum_fusion.3), channel_id=1, source_target_pairs={{0,2},{2,0},{4,6},{6,4},{8,10},{10,8},{12,14},{14,12},{16,18},{18,... | collective-permute-start | bytes 3538952 | tf_op jit(solution)/shard_map/ppermute | solution.py:56
  86.3 50.7 %collective-permute-start.10 = (bf16[192,3072]{1,0:T(8,128)(2,1)S(1)}, bf16[192,3072]{1,0:T(8,128)(2,1)S(1)}, u32[]{:S(2)}, u32[]{:S(2)}) collective-permute-start(bf16[192,3072]{1,0:T(8,128)(2,1)S(1)} %pad_maximum_fusion.3), channel_id=1, source_target_pairs={{0,4},{2,6},{4,0},{6,2},{8,12},{10,14},{12,8},{14,10},{16,20},{18,... | collective-permute-start | bytes 3538952 | tf_op jit(solution)/shard_map/ppermute | solution.py:56
  96.0 38.5 %collective-permute-start.18 = (bf16[192,1536]{1,0:T(8,128)(2,1)}, bf16[192,1536]{1,0:T(8,128)(2,1)}, u32[]{:S(2)}, u32[]{:S(2)}) collective-permute-start(bf16[192,1536]{1,0:T(8,128)(2,1)} %constant_dynamic-update-slice_fusion.2), channel_id=1, source_target_pairs={{0,8},{2,10},{4,12},{6,14},{8,24},{10,26},{12,28},{14,30},{16,0},{... | collective-permute-start | bytes 1769480 | tf_op jit(solution)/shard_map/ppermute | solution.py:56
  120.8 36.0 %collective-permute-start.8 = (bf16[1024,768]{0,1:T(8,128)(2,1)S(1)}, bf16[1024,768]{0,1:T(8,128)(2,1)S(1)}, u32[]{:S(2)}, u32[]{:S(2)}) collective-permute-start(bf16[1024,768]{0,1:T(8,128)(2,1)S(1)} %convolution_convert_fusion.5), channel_id=1, source_target_pairs={{0,1},{1,0},{2,3},{3,2},{4,5},{5,4},{6,7},{7,6},{8,9},{9,8},{10,11... | collective-permute-start | bytes 4718600 | tf_op jit(solution)/shard_map/ppermute | solution.py:357
  153.8 27.6 %collective-permute-start.15 = (bf16[192,1536]{1,0:T(8,128)(2,1)S(1)}, bf16[192,1536]{1,0:T(8,128)(2,1)S(1)}, u32[]{:S(2)}, u32[]{:S(2)}) collective-permute-start(bf16[192,1536]{1,0:T(8,128)(2,1)S(1)} %copy-done.17), channel_id=1, source_target_pairs={{0,2},{2,0},{4,6},{6,4},{8,10},{10,8},{12,14},{14,12},{16,18},{18,... | collective-permute-start | bytes 1769480 | tf_op jit(solution)/shard_map/ppermute | solution.py:56
  155.3 27.7 %collective-permute-start.14 = (bf16[192,1536]{1,0:T(8,128)(2,1)S(1)}, bf16[192,1536]{1,0:T(8,128)(2,1)S(1)}, u32[]{:S(2)}, u32[]{:S(2)}) collective-permute-start(bf16[192,1536]{1,0:T(8,128)(2,1)S(1)} %copy-done.17), channel_id=1, source_target_pairs={{0,4},{2,6},{4,0},{6,2},{8,12},{10,14},{12,8},{14,10},{16,20},{18,... | collective-permute-start | bytes 1769480 | tf_op jit(solution)/shard_map/ppermute | solution.py:56
  181.4 27.1 %collective-permute-start.17 = (bf16[96,1536]{1,0:T(8,128)(2,1)S(1)}, bf16[96,1536]{1,0:T(8,128)(2,1)S(1)}, u32[]{:S(2)}, u32[]{:S(2)}) collective-permute-start(bf16[96,1536]{1,0:T(8,128)(2,1)S(1)} %slice.389), channel_id=1, source_target_pairs={{0,4},{2,6},{4,0},{6,2},{8,12},{10,14},{12,8},{14,10},{16,20},{18,... | collective-permute-start | bytes 884744 | tf_op jit(solution)/shard_map/ppermute | solution.py:56
  183.0 25.5 %collective-permute-start.16 = (bf16[96,1536]{1,0:T(8,128)(2,1)S(1)}, bf16[96,1536]{1,0:T(8,128)(2,1)S(1)}, u32[]{:S(2)}, u32[]{:S(2)}) collective-permute-start(bf16[96,1536]{1,0:T(8,128)(2,1)S(1)} %slice.388), channel_id=1, source_target_pairs={{0,2},{2,0},{4,6},{6,4},{8,10},{10,8},{12,14},{14,12},{16,18},{18,... | collective-permute-start | bytes 884744 | tf_op jit(solution)/shard_map/ppermute | solution.py:56
  205.2 38.9 %collective-permute-start.30 = (bf16[192,3072]{1,0:T(8,128)(2,1)}, bf16[192,3072]{1,0:T(8,128)(2,1)}, u32[]{:S(2)}, u32[]{:S(2)}) collective-permute-start(bf16[192,3072]{1,0:T(8,128)(2,1)} %fusion.95), channel_id=1, source_target_pairs={{0,4},{2,6},{4,0},{6,2},{8,12},{10,14},{12,8},{14,10},{16,20},{18,... | collective-permute-start | bytes 3538952 | tf_op jit(solution)/shard_map/ppermute | solution.py:56
  208.0 36.2 %collective-permute-start.29 = (bf16[192,3072]{1,0:T(8,128)(2,1)}, bf16[192,3072]{1,0:T(8,128)(2,1)}, u32[]{:S(2)}, u32[]{:S(2)}) collective-permute-start(bf16[192,3072]{1,0:T(8,128)(2,1)} %pad_maximum_fusion.6), channel_id=1, source_target_pairs={{0,2},{2,0},{4,6},{6,4},{8,10},{10,8},{12,14},{14,12},{16,18},{18,... | collective-permute-start | bytes 3538952 | tf_op jit(solution)/shard_map/ppermute | solution.py:56
  222.8 47.2 %collective-permute-start.21 = (bf16[1024,768]{0,1:T(8,128)(2,1)S(1)}, bf16[1024,768]{0,1:T(8,128)(2,1)}, u32[]{:S(2)}, u32[]{:S(2)}) collective-permute-start(bf16[1024,768]{0,1:T(8,128)(2,1)S(1)} %fusion.58), channel_id=1, source_target_pairs={{0,1},{1,0},{2,3},{3,2},{4,5},{5,4},{6,7},{7,6},{8,9},{9,8},{10,11... | collective-permute-start | bytes 4718600 | tf_op jit(solution)/shard_map/ppermute | solution.py:357
  242.7 31.6 %collective-permute-start.24 = (bf16[1024,768]{0,1:T(8,128)(2,1)S(1)}, bf16[1024,768]{0,1:T(8,128)(2,1)S(1)}, u32[]{:S(2)}, u32[]{:S(2)}) collective-permute-start(bf16[1024,768]{0,1:T(8,128)(2,1)S(1)} %fusion.59), channel_id=1, source_target_pairs={{0,1},{1,0},{2,3},{3,2},{4,5},{5,4},{6,7},{7,6},{8,9},{9,8},{10,11... | collective-permute-start | bytes 4718600 | tf_op jit(solution)/shard_map/ppermute | solution.py:357
  246.4 22.1 %collective-permute-start.31 = (bf16[48,3072]{1,0:T(8,128)(2,1)S(1)}, bf16[48,3072]{1,0:T(8,128)(2,1)S(1)}, u32[]{:S(2)}, u32[]{:S(2)}) collective-permute-start(bf16[48,3072]{1,0:T(8,128)(2,1)S(1)} %get-tuple-element.105), channel_id=1, source_target_pairs={{0,16},{2,18},{4,20},{6,22},{8,0},{10,2},{12,4},{14,6},{16,24},{18... | collective-permute-start | bytes 884744 | tf_op jit(solution)/shard_map/ppermute | solution.py:56
  246.5 22.0 %collective-permute-start.33 = (bf16[48,3072]{1,0:T(8,128)(2,1)S(1)}, bf16[48,3072]{1,0:T(8,128)(2,1)S(1)}, u32[]{:S(2)}, u32[]{:S(2)}) collective-permute-start(bf16[48,3072]{1,0:T(8,128)(2,1)S(1)} %get-tuple-element.106), channel_id=1, source_target_pairs={{0,8},{2,10},{4,12},{6,14},{8,24},{10,26},{12,28},{14,30},{16,0},{... | collective-permute-start | bytes 884744 | tf_op jit(solution)/shard_map/ppermute | solution.py:56
  268.5 42.4 %collective-permute-start.26 = (bf16[192,3072]{1,0:T(8,128)(2,1)}, bf16[192,3072]{1,0:T(8,128)(2,1)}, u32[]{:S(2)}, u32[]{:S(2)}) collective-permute-start(bf16[192,3072]{1,0:T(8,128)(2,1)} %pad_maximum_fusion.4), channel_id=1, source_target_pairs={{0,2},{2,0},{4,6},{6,4},{8,10},{10,8},{12,14},{14,12},{16,18},{18,... | collective-permute-start | bytes 3538952 | tf_op jit(solution)/shard_map/ppermute | solution.py:56
  268.5 42.4 %collective-permute-start.28 = (bf16[192,3072]{1,0:T(8,128)(2,1)}, bf16[192,3072]{1,0:T(8,128)(2,1)}, u32[]{:S(2)}, u32[]{:S(2)}) collective-permute-start(bf16[192,3072]{1,0:T(8,128)(2,1)} %pad_maximum_fusion.5), channel_id=1, source_target_pairs={{0,4},{2,6},{4,0},{6,2},{8,12},{10,14},{12,8},{14,10},{16,20},{18,... | collective-permute-start | bytes 3538952 | tf_op jit(solution)/shard_map/ppermute | solution.py:56
  331.0 21.7 %collective-permute-start.37 = (bf16[48,3072]{1,0:T(8,128)(2,1)S(1)}, bf16[48,3072]{1,0:T(8,128)(2,1)}, u32[]{:S(2)}, u32[]{:S(2)}) collective-permute-start(bf16[48,3072]{1,0:T(8,128)(2,1)S(1)} %get-tuple-element.104), channel_id=1, source_target_pairs={{0,24},{2,26},{4,28},{6,30},{8,16},{10,18},{12,20},{14,22},{16,8},... | collective-permute-start | bytes 884744 | tf_op jit(solution)/shard_map/ppermute | solution.py:56
  (69 other events, 737.8 us)
